TPU v7x, 8 devices: a whole 2x2x1 slice. The times are simulated.
8 devices in a mesh: req: 2 (over z, y), dap: 4 (over x, core).
Axes of the slice: x: 2, y: 2, z: 1, core: 2. Of those that a mesh axis runs over, the one named last changes fastest.
Arguments:
- msa_act: bfloat16 [512, 256, 256], P(('req', 'dap')), parts along dimension 0
- pair_act: bfloat16 [512, 256, 128], P(('req', 'dap')), parts along dimension 0
- msa_mask: int32 [512, 256], P(('req', 'dap')), parts along dimension 0
- pair_mask: int32 [512, 256], P(('req', 'dap')), parts along dimension 0
- row_qkvg: bfloat16 [2, 256, 1024], replicated
- row_bias: bfloat16 [2, 128, 8], replicated
- row_out: bfloat16 [2, 256, 256], replicated
- col_qkvg: bfloat16 [2, 256, 1024], replicated
- col_out: bfloat16 [2, 256, 256], replicated
- mtr_in: bfloat16 [2, 256, 1024], replicated
- mtr_out: bfloat16 [2, 1024, 256], replicated
- opm_proj: bfloat16 [2, 256, 64], replicated
- opm_out: bfloat16 [2, 1024, 128], replicated
- tmo_proj: bfloat16 [2, 128, 640], replicated
- tmo_out: bfloat16 [2, 128, 128], replicated
- tmi_proj: bfloat16 [2, 128, 640], replicated
- tmi_out: bfloat16 [2, 128, 128], replicated
- tas_qkvg: bfloat16 [2, 128, 512], replicated
- tas_bias: bfloat16 [2, 128, 4], replicated
- tas_out: bfloat16 [2, 128, 128], replicated
- tae_qkvg: bfloat16 [2, 128, 512], replicated
- tae_bias: bfloat16 [2, 128, 4], replicated
- tae_out: bfloat16 [2, 128, 128], replicated
- ptr_in: bfloat16 [2, 128, 512], replicated
- ptr_out: bfloat16 [2, 512, 128], replicated
Outputs:
- output 1: bfloat16 [512, 256, 256], P(('req', 'dap')), parts along dimension 0
- output 2: bfloat16 [512, 256, 128], P(('req', 'dap')), parts along dimension 0
There are 2 independent parts. A program takes and returns all parts, laid end to end along the dimension named above; an argument that names none is the same for every part.
All inputs are finite; a program needn't handle non-finite values.
Results may differ from a plain program's by a relative error of at most 0.02.
Values are sent between devices in bfloat16 or wider.
A program may use at most 1 GiB of HBM per device.

v0:
```python
import jax
import jax.numpy as jnp
from jax import lax
from jax.sharding import PartitionSpec as P

GROUP_AXIS = 'dap'
PARTS_AXIS = 'req'
MASKED_LOGIT = -1e9


def layer_norm(x):
    values = x.astype(jnp.float32)
    centered = values - jnp.mean(values, axis=-1, keepdims=True)
    variance = jnp.mean(centered * centered, axis=-1, keepdims=True)
    return (centered * lax.rsqrt(variance + 1e-5)).astype(jnp.bfloat16)


def residual(x, update):
    return (x.astype(jnp.float32) + update).astype(jnp.bfloat16)


def dense(x, weight):
    return jnp.einsum('...c,cf->...f', x, weight, preferred_element_type=jnp.float32)


def attend(queries, gate_raw, keyvals, num_heads, pair_bias, key_mask, w_out):
    n_batch, q_len, head_width = queries.shape
    k_len = keyvals.shape[1]
    head_dim = head_width // num_heads
    q_heads = queries.reshape(n_batch, q_len, num_heads, head_dim)
    k_heads = keyvals[..., :head_width].reshape(n_batch, k_len, num_heads, head_dim)
    v_heads = keyvals[..., head_width:].reshape(n_batch, k_len, num_heads, head_dim)
    logits = jnp.einsum('bqhd,bkhd->bhqk', q_heads, k_heads, preferred_element_type=jnp.float32) * head_dim ** -0.5
    if pair_bias is not None:
        logits = logits + pair_bias.astype(jnp.float32)
    logits = jnp.where(key_mask[:, None, None, :] > 0, logits, MASKED_LOGIT)
    attn_prob = jax.nn.softmax(logits, axis=-1).astype(jnp.bfloat16)
    attended = jnp.einsum('bhqk,bkhd->bqhd', attn_prob, v_heads, preferred_element_type=jnp.float32)
    gated = (attended.reshape(n_batch, q_len, head_width) * jax.nn.sigmoid(gate_raw.astype(jnp.float32))).astype(jnp.bfloat16)
    return dense(gated, w_out)


def self_attention(x_norm, w_qkvg, num_heads, pair_bias, key_mask, w_out):
    head_width = w_out.shape[0]
    projected = dense(x_norm, w_qkvg).astype(jnp.bfloat16)
    return attend(projected[..., :head_width], projected[..., 3 * head_width:], projected[..., head_width:3 * head_width], num_heads, pair_bias, key_mask, w_out)


def head_bias(pair_norm, w_bias):
    return jnp.einsum('ijc,ch->hij', pair_norm, w_bias, preferred_element_type=jnp.float32).astype(jnp.bfloat16)


def transition(x, w_in, w_out):
    hidden = jnp.maximum(dense(layer_norm(x), w_in), 0.0).astype(jnp.bfloat16)
    return dense(hidden, w_out)


def outer_update(array_b7, res_mask, full_mask, w_proj, w_out):
    opm_dim = w_proj.shape[1] // 2
    projected = dense(layer_norm(array_b7), w_proj).astype(jnp.bfloat16)
    mask_bf = res_mask.astype(jnp.bfloat16)[:, :, None]
    left_act = projected[..., :opm_dim] * mask_bf
    right_act = projected[..., opm_dim:] * mask_bf
    right_full = lax.all_gather(right_act, GROUP_AXIS, axis=1, tiled=True)
    outer_prod = jnp.einsum('sic,sje->ijce', left_act, right_full, preferred_element_type=jnp.float32).astype(jnp.bfloat16)
    n_rows, n_cols = outer_prod.shape[:2]
    update = dense(outer_prod.reshape(n_rows, n_cols, opm_dim * opm_dim), w_out)
    overlap = jnp.einsum('si,sj->ij', res_mask.astype(jnp.float32), full_mask.astype(jnp.float32))
    return update / (1e-3 + overlap)[:, :, None]


def tri_gates(pair_rows, mask_rows, w_proj):
    tri_dim = (w_proj.shape[1] - pair_rows.shape[-1]) // 4
    projected = dense(layer_norm(pair_rows), w_proj)
    mask_f = mask_rows.astype(jnp.float32)[:, :, None]
    left_act = (mask_f * jax.nn.sigmoid(projected[..., 2 * tri_dim:3 * tri_dim]) * projected[..., :tri_dim]).astype(jnp.bfloat16)
    right_act = (mask_f * jax.nn.sigmoid(projected[..., 3 * tri_dim:4 * tri_dim]) * projected[..., tri_dim:2 * tri_dim]).astype(jnp.bfloat16)
    gate_act = jax.nn.sigmoid(projected[..., 4 * tri_dim:])
    return left_act, right_act, gate_act


def tri_finish(product, gate_act, w_out):
    return gate_act * dense(layer_norm(product), w_out)


def tri_attention(pair_rows, mask_rows, w_qkvg, w_bias, w_out):
    pair_norm = layer_norm(pair_rows)
    bias_full = lax.all_gather(head_bias(pair_norm, w_bias), GROUP_AXIS, axis=1, tiled=True)
    return self_attention(pair_norm, w_qkvg, w_bias.shape[1], bias_full, mask_rows, w_out)


def pair_stack(pair_loc, pair_mask, pair_mask_t, pair_w):
    (tmo_proj, tmo_out, tmi_proj, tmi_out, tas_qkvg, tas_bias, tas_out,
     tae_qkvg, tae_bias, tae_out, ptr_in, ptr_out) = pair_w
    left_act, right_act, gate_act = tri_gates(pair_loc, pair_mask, tmo_proj)
    right_full = lax.all_gather(right_act, GROUP_AXIS, axis=0, tiled=True)
    product = jnp.einsum('ikc,jkc->ijc', left_act, right_full, preferred_element_type=jnp.float32)
    pair_loc = residual(pair_loc, tri_finish(product, gate_act, tmo_out))
    left_act, right_act, gate_act = tri_gates(pair_loc, pair_mask, tmi_proj)
    left_cols = lax.all_to_all(left_act, GROUP_AXIS, 1, 0, tiled=True)
    right_full = lax.all_gather(right_act, GROUP_AXIS, axis=0, tiled=True)
    product = jnp.einsum('kic,kjc->ijc', left_cols, right_full, preferred_element_type=jnp.float32)
    pair_loc = residual(pair_loc, tri_finish(product, gate_act, tmi_out))
    pair_loc = residual(pair_loc, tri_attention(pair_loc, pair_mask, tas_qkvg, tas_bias, tas_out))
    pair_cols = lax.all_to_all(pair_loc, GROUP_AXIS, 1, 0, tiled=True)
    pair_t = jnp.swapaxes(pair_cols, 0, 1)
    pair_t = residual(pair_t, tri_attention(pair_t, pair_mask_t, tae_qkvg, tae_bias, tae_out))
    pair_loc = lax.all_to_all(jnp.swapaxes(pair_t, 0, 1), GROUP_AXIS, 0, 1, tiled=True)
    return residual(pair_loc, transition(pair_loc, ptr_in, ptr_out))


def evoformer_block(value_a7, pair_loc, full_mask, full_pair_mask, layer_w):
    (row_qkvg, row_bias, row_out, col_qkvg, col_out, mtr_in, mtr_out, opm_proj, opm_out) = layer_w[:9]
    shard_idx = lax.axis_index(GROUP_AXIS)
    seq_loc = value_a7.shape[0]
    res_loc = pair_loc.shape[0]
    seq_mask = lax.dynamic_slice_in_dim(full_mask, shard_idx * seq_loc, seq_loc, 0)
    res_mask = lax.dynamic_slice_in_dim(full_mask, shard_idx * res_loc, res_loc, 1)
    pair_mask = lax.dynamic_slice_in_dim(full_pair_mask, shard_idx * res_loc, res_loc, 0)
    pair_mask_t = lax.dynamic_slice_in_dim(full_pair_mask, shard_idx * res_loc, res_loc, 1).T
    value_a9 = row_bias.shape[1]
    row_bias_full = lax.all_gather(head_bias(layer_norm(pair_loc), row_bias), GROUP_AXIS, axis=1, tiled=True)
    value_a7 = residual(value_a7, self_attention(layer_norm(value_a7), row_qkvg, value_a9, row_bias_full, seq_mask, row_out))
    array_b7 = lax.all_to_all(value_a7, GROUP_AXIS, 1, 0, tiled=True)
    col_norm = jnp.swapaxes(layer_norm(array_b7), 0, 1)
    col_update = self_attention(col_norm, col_qkvg, value_a9, None, res_mask.T, col_out)
    array_b7 = residual(array_b7, jnp.swapaxes(col_update, 0, 1))
    array_b7 = residual(array_b7, transition(array_b7, mtr_in, mtr_out))
    pair_loc = residual(pair_loc, outer_update(array_b7, res_mask, full_mask, opm_proj, opm_out))
    pair_loc = pair_stack(pair_loc, pair_mask, pair_mask_t, layer_w[9:])
    value_a7 = lax.all_to_all(array_b7, GROUP_AXIS, 0, 1, tiled=True)
    return value_a7, pair_loc


def solution(mesh):
    row_spec = P((PARTS_AXIS, GROUP_AXIS))

    def local_body(value_a7, pair_loc, value_a12, pair_mask_loc, *weights):
        full_mask = lax.all_gather(value_a12, GROUP_AXIS, axis=0, tiled=True)
        full_pair_mask = lax.all_gather(pair_mask_loc, GROUP_AXIS, axis=0, tiled=True)
        for layer_idx in range(weights[0].shape[0]):
            layer_w = tuple(weight[layer_idx] for weight in weights)
            value_a7, pair_loc = evoformer_block(value_a7, pair_loc, full_mask, full_pair_mask, layer_w)
        return value_a7, pair_loc

    def run_blocks(*arrays):
        n_weights = len(arrays) - 4
        return jax.shard_map(local_body, mesh=mesh, in_specs=(row_spec,) * 4 + (P(),) * n_weights, out_specs=(row_spec, row_spec), check_vma=False)(*arrays)

    return run_blocks
```

profile of v0, /device:TPU:0, one launch (start us, length us, event | category | flops | bytes accessed | tf_op | source)
XLA Modules:
  0.0 3324.2 jit_solution(76055681285189870)
XLA Ops:
  115.9 60.4 %fusion.470 = (f32[64,8,256]{2,1,0:T(8,128)S(1)}, f32[64,8,256,256]{2,3,1,0:T(8,128)}) fusion(f32[8,256,256]{1,2,0:T(8,128)S(1)} %copy.1217, pred[64,256]{1,0:T(8,128)(4,1)S(1)} %dynamic-slice_compare_fusion, bf16[64,256,8,32]{1,3,2,0:T(8,128)(2,1)} %bitcast.544, bf16[64,256,8,32]{1,3,2,0:T(8,128)(2,1)} %bitcast.546), kind=kOutput, calls=%fused_computation.618 | convolution fusion | flops 2315256064 | bytes 153632768 | tf_op jit(solution)/shard_map/sub | solution.py:37
  176.3 49.8 %fusion.26 = f32[64,8,32,256]{3,2,1,0:T(8,128)} fusion(bf16[64,256,8,32]{1,3,2,0:T(8,128)(2,1)} %bitcast.545, f32[64,8,256,256]{2,3,1,0:T(8,128)} %get-tuple-element.43, f32[64,8,256]{2,1,0:T(8,128)S(1)} %get-tuple-element.42), kind=kOutput, calls=%fused_computation.52 | convolution fusion | flops 2214592512 | bytes 159907840 | tf_op jit(solution)/shard_map/bhqk,bkhd->bqhd/dot_general | solution.py:38
  277.9 96.1 %all_gather.45 = s32[256,256]{1,0:T(8,128)S(1)} all-gather(s32[64,256]{1,0:T(8,128)S(1)} %copy-done.52), channel_id=1, replica_groups=mesh['req'=2,'dap'=4] {'dap'}, dimensions={0}, use_global_device_ids=true | all-gather | bytes 327680 | tf_op jit(solution)/shard_map/all_gather | solution.py:140
  413.3 45.0 %convolution_convert_fusion.2 = bf16[64,256,1024]{2,1,0:T(8,128)(2,1)} fusion(bf16[64,256,256]{2,0,1:T(8,128)(2,1)} %fusion.149, bf16[2,256,1024]{2,1,0:T(8,128)(2,1)S(1)} %copy-done.31), kind=kOutput, calls=%fused_computation.103 | convolution fusion | flops 8606711808 | bytes 42467328 | tf_op jit(solution)/shard_map/...c,cf->...f/dot_general | solution.py:23
  511.3 57.7 %fusion.471 = (f32[64,8,256]{2,1,0:T(8,128)S(1)}, f32[64,8,256,256]{2,3,1,0:T(8,128)}) fusion(pred[64,256]{1,0:T(8,128)(4,1)S(1)} %compare_bitcast_fusion.1, bf16[64,256,8,32]{1,3,2,0:T(8,128)(2,1)} %bitcast.551, bf16[64,256,8,32]{1,3,2,0:T(8,128)(2,1)} %bitcast.554), kind=kOutput, calls=%fused_computation.619 | convolution fusion | flops 2281701632 | bytes 151535616 | tf_op jit(solution)/shard_map/sub | solution.py:37
  569.0 49.7 %fusion.27 = f32[64,8,32,256]{3,2,1,0:T(8,128)} fusion(bf16[64,256,8,32]{1,3,2,0:T(8,128)(2,1)} %bitcast.555, f32[64,8,256,256]{2,3,1,0:T(8,128)} %get-tuple-element.45, f32[64,8,256]{2,1,0:T(8,128)S(1)} %get-tuple-element.44), kind=kOutput, calls=%fused_computation.53 | convolution fusion | flops 2214592512 | bytes 159907840 | tf_op jit(solution)/shard_map/bhqk,bkhd->bqhd/dot_general | solution.py:38
  711.2 31.7 all-gather.11.cloned.1.call-done
  763.3 31.2 copy.1250
  851.0 104.3 %all-gather.13.cloned.1.call-done = bf16[256,256,128]{2,1,0:T(8,128)(2,1)} async-done(((bf16[64,256,128]{2,1,0:T(8,128)(2,1)}), bf16[256,256,128]{2,1,0:T(8,128)(2,1)}) %all-gather.13.cloned.1.call-update) | async-done | bytes 16777232 | tf_op jit(solution)/shard_map/all_gather | solution.py:96
  1073.9 80.2 %all-to-all-done.2 = bf16[64,256,128]{2,0,1:T(8,128)(2,1)} async-done(((bf16[64,256,128]{2,0,1:T(8,128)(2,1)}), bf16[64,256,128]{2,0,1:T(8,128)(2,1)}, u32[]{:S(2)}, u32[]{:S(2)}) %all-to-all-start.2) | async-done | bytes 4194336 | tf_op jit(solution)/shard_map/all_to_all | solution.py:100
  1174.2 59.0 %all-gather.15.cloned.1.call-done = bf16[256,256,128]{2,1,0:T(8,128)(2,1)} async-done(((bf16[64,256,128]{2,1,0:T(8,128)(2,1)}), bf16[256,256,128]{2,1,0:T(8,128)(2,1)}) %all-gather.15.cloned.1.call-update) | async-done | bytes 16777232 | tf_op jit(solution)/shard_map/all_gather | solution.py:101
  1312.2 31.9 fusion.476
  1344.1 26.4 fusion.54
  1398.4 41.3 %all-to-all-done.3 = bf16[64,256,128]{2,0,1:T(8,128)(2,1)} async-done(((bf16[64,256,128]{2,0,1:T(8,128)(2,1)}), bf16[64,256,128]{2,0,1:T(8,128)(2,1)}, u32[]{:S(2)}, u32[]{:S(2)}) %all-to-all-start.3) | async-done | bytes 4194336 | tf_op jit(solution)/shard_map/all_to_all | solution.py:105
  1492.1 31.9 fusion.477
  1524.0 26.4 fusion.55
  1756.1 60.4 %fusion.480 = (f32[64,8,256]{2,1,0:T(8,128)S(1)}, f32[64,8,256,256]{2,3,1,0:T(8,128)}) fusion(f32[8,256,256]{1,2,0:T(8,128)S(1)} %copy.1305, pred[64,256]{1,0:T(8,128)(4,1)S(1)} %copy-done.60, bf16[64,256,8,32]{1,3,2,0:T(8,128)(2,1)} %bitcast.547, bf16[64,256,8,32]{1,3,2,0:T(8,128)(2,1)} %bitcast.549), kind=kOutput, calls=%fused_computation.622 | convolution fusion | flops 2315256064 | bytes 153632768 | tf_op jit(solution)/shard_map/sub | solution.py:37
  1816.5 49.7 %fusion.28 = f32[64,8,32,256]{3,2,1,0:T(8,128)} fusion(bf16[64,256,8,32]{1,3,2,0:T(8,128)(2,1)} %bitcast.548, f32[64,8,256,256]{2,3,1,0:T(8,128)} %get-tuple-element.67, f32[64,8,256]{2,1,0:T(8,128)S(1)} %get-tuple-element.66), kind=kOutput, calls=%fused_computation.54 | convolution fusion | flops 2214592512 | bytes 159907840 | tf_op jit(solution)/shard_map/bhqk,bkhd->bqhd/dot_general | solution.py:38
  1913.7 97.2 %all_to_all.117 = bf16[64,256,256]{2,0,1:T(8,128)(2,1)S(1)} all-to-all(bf16[64,256,256]{2,0,1:T(8,128)(2,1)} %copy.1308), channel_id=1, replica_groups=mesh['req'=2,'dap'=4] {'dap'}, dimensions={1} | all-to-all | bytes 16777216 | tf_op jit(solution)/shard_map/all_to_all | solution.py:124
  2057.5 45.3 %convolution_convert_fusion = bf16[64,256,1024]{2,1,0:T(8,128)(2,1)} fusion(bf16[64,256,256]{2,0,1:T(8,128)(2,1)} %fusion.150, bf16[2,256,1024]{2,1,0:T(8,128)(2,1)S(1)} %copy-done.32), kind=kOutput, calls=%fused_computation.101 | convolution fusion | flops 8606711808 | bytes 42467328 | tf_op jit(solution)/shard_map/...c,cf->...f/dot_general | solution.py:23
  2155.7 57.7 %fusion.481 = (f32[64,8,256]{2,1,0:T(8,128)S(1)}, f32[64,8,256,256]{2,3,1,0:T(8,128)}) fusion(pred[64,256]{1,0:T(8,128)(4,1)S(1)} %copy-done.58, bf16[64,256,8,32]{1,3,2,0:T(8,128)(2,1)} %bitcast.550, bf16[64,256,8,32]{1,3,2,0:T(8,128)(2,1)} %bitcast.552), kind=kOutput, calls=%fused_computation.623 | convolution fusion | flops 2281701632 | bytes 151535616 | tf_op jit(solution)/shard_map/sub | solution.py:37
  2213.4 49.7 %fusion.29 = f32[64,8,32,256]{3,2,1,0:T(8,128)} fusion(bf16[64,256,8,32]{1,3,2,0:T(8,128)(2,1)} %bitcast.553, f32[64,8,256,256]{2,3,1,0:T(8,128)} %get-tuple-element.69, f32[64,8,256]{2,1,0:T(8,128)S(1)} %get-tuple-element.68), kind=kOutput, calls=%fused_computation.55 | convolution fusion | flops 2214592512 | bytes 159907840 | tf_op jit(solution)/shard_map/bhqk,bkhd->bqhd/dot_general | solution.py:38
  2354.4 31.8 all-gather.19.cloned.1.call-done
  2406.9 31.3 copy.1333
  2494.6 104.3 %all-gather.21.cloned.1.call-done = bf16[256,256,128]{2,1,0:T(8,128)(2,1)} async-done(((bf16[64,256,128]{2,1,0:T(8,128)(2,1)}), bf16[256,256,128]{2,1,0:T(8,128)(2,1)}) %all-gather.21.cloned.1.call-update) | async-done | bytes 16777232 | tf_op jit(solution)/shard_map/all_gather | solution.py:96
  2699.3 97.5 %all_to_all.118 = bf16[64,256,128]{2,0,1:T(8,128)(2,1)S(1)} all-to-all(bf16[64,256,128]{2,0,1:T(8,128)(2,1)} %copy.1354), channel_id=1, replica_groups=mesh['req'=2,'dap'=4] {'dap'}, dimensions={1} | all-to-all | bytes 8388608 | tf_op jit(solution)/shard_map/all_to_all | solution.py:100
  2808.8 33.3 %all-gather.23.cloned.1.call-done = bf16[256,256,128]{2,1,0:T(8,128)(2,1)} async-done(((bf16[64,256,128]{2,1,0:T(8,128)(2,1)}), bf16[256,256,128]{2,1,0:T(8,128)(2,1)}) %all-gather.23.cloned.1.call-update) | async-done | bytes 16777232 | tf_op jit(solution)/shard_map/all_gather | solution.py:101
  2917.1 31.9 fusion.486
  3008.7 35.7 %all-to-all-done.8 = bf16[64,256,128]{2,0,1:T(8,128)(2,1)} async-done(((bf16[64,256,128]{2,0,1:T(8,128)(2,1)}), bf16[64,256,128]{2,0,1:T(8,128)(2,1)}, u32[]{:S(2)}, u32[]{:S(2)}) %all-to-all-start.8) | async-done | bytes 4194336 | tf_op jit(solution)/shard_map/all_to_all | solution.py:105
  3093.0 55.6 %all_gather.55 = bf16[4,256,256]{2,0,1:T(4,128)(2,1)S(1)} all-gather(bf16[4,64,256]{2,0,1:T(4,128)(2,1)S(1)} %fusion.323), channel_id=1, replica_groups=mesh['req'=2,'dap'=4] {'dap'}, dimensions={1}, use_global_device_ids=true | all-gather | bytes 655360 | tf_op jit(solution)/shard_map/all_gather | solution.py:88
  3149.1 31.9 fusion.487
  3236.2 39.4 %all-to-all-done.9 = bf16[256,64,128]{2,1,0:T(8,128)(2,1)} async-done(((bf16[256,64,128]{2,1,0:T(8,128)(2,1)}), bf16[256,64,128]{2,1,0:T(8,128)(2,1)}, u32[]{:S(2)}, u32[]{:S(2)}) %all-to-all-start.9) | async-done | bytes 4194336 | tf_op jit(solution)/shard_map/all_to_all | solution.py:108
  (447 shorter events, 1632.3 us)
Async XLA Ops:
  7.2 106.8 %all-gather.9.cloned.1.call-start = ((), (), s32[]{:S(2)}) async-start(), calls=%async_computation.10 | async-start | bytes 1310720 | tf_op jit(solution)/shard_map/all_gather | solution.py:122
  114.0 62.3 %copy-start.59 = (pred[64,256]{1,0:T(8,128)(4,1)}, pred[64,256]{1,0:T(8,128)(4,1)S(1)}, u32[]{:S(2)}) copy-start(pred[64,256]{1,0:T(8,128)(4,1)S(1)} %dynamic-slice_compare_fusion) | copy-start | bytes 49156
  272.0 102.0 %copy-start.24 = (s32[256,256]{1,0:T(8,128)S(1)}, s32[256,256]{1,0:T(8,128)}, u32[]{:S(2)}) copy-start(s32[256,256]{1,0:T(8,128)} %copy-done.23) | copy-start | bytes 786436
  272.0 103.5 %all-to-all-start = ((bf16[64,256,256]{2,0,1:T(8,128)(2,1)}), bf16[64,256,256]{2,0,1:T(8,128)(2,1)}, u32[]{:S(2)}, u32[]{:S(2)}) async-start(bf16[64,256,256]{2,0,1:T(8,128)(2,1)} %copy.1220), calls=%async_computation | async-start | bytes 16777216 | tf_op jit(solution)/shard_map/all_to_all | solution.py:124
  277.8 465.2 %all-gather.11.cloned.1.call-start = ((), (), s32[]{:S(2)}) async-start(), calls=%async_computation.11 | async-start | bytes 5242880 | tf_op jit(solution)/shard_map/all_gather | solution.py:64
  375.5 135.8 %copy-start.57 = (pred[64,256]{1,0:T(8,128)(4,1)}, pred[64,256]{1,0:T(8,128)(4,1)S(1)}, u32[]{:S(2)}) copy-start(pred[64,256]{1,0:T(8,128)(4,1)S(1)} %compare_bitcast_fusion.1) | copy-start | bytes 49156
  636.2 17.7 copy-start.69
  710.2 245.1 %all-gather.13.cloned.1.call-start = ((), (), s32[]{:S(2)}) async-start(), calls=%async_computation.12 | async-start | bytes 20971520 | tf_op jit(solution)/shard_map/all_gather | solution.py:96
  711.1 315.1 %copy-start.26 = (f32[64,256]{1,0:T(8,128)}, f32[64,256]{1,0:T(8,128)S(1)}, u32[]{:S(2)}) copy-start(f32[64,256]{1,0:T(8,128)S(1)} %dynamic-slice_convert_fusion) | copy-start | bytes 196612
  711.2 83.3 %copy-start.53 = (f32[64,256]{1,0:T(8,128)}, f32[64,256]{1,0:T(8,128)S(1)}, u32[]{:S(2)}) copy-start(f32[64,256]{1,0:T(8,128)S(1)} %convolution_add_fusion) | copy-start | bytes 196612
  809.3 18.3 copy-start.19
  851.0 382.2 %all-gather.15.cloned.1.call-start = ((), (), s32[]{:S(2)}) async-start(), calls=%async_computation.13 | async-start | bytes 20971520 | tf_op jit(solution)/shard_map/all_gather | solution.py:101
  1007.6 18.6 copy-start.13
  1056.0 98.1 %all-to-all-start.2 = ((bf16[64,256,128]{2,0,1:T(8,128)(2,1)}), bf16[64,256,128]{2,0,1:T(8,128)(2,1)}, u32[]{:S(2)}, u32[]{:S(2)}) async-start(bf16[64,256,128]{2,0,1:T(8,128)(2,1)} %copy.1271), calls=%async_computation.2 | async-start | bytes 8388608 | tf_op jit(solution)/shard_map/all_to_all | solution.py:100
  1061.7 250.5 %copy-start.55 = (pred[64,256]{1,0:T(8,128)(4,1)}, pred[64,256]{1,0:T(8,128)(4,1)S(1)}, u32[]{:S(2)}) copy-start(pred[64,256]{1,0:T(8,128)(4,1)S(1)} %dynamic-slice_compare_fusion.1) | copy-start | bytes 49156
  1154.1 232.9 %all-to-all-start.1 = ((bf16[256,64,256]{2,1,0:T(8,128)(2,1)}), bf16[256,64,256]{2,1,0:T(8,128)(2,1)}, u32[]{:S(2)}, u32[]{:S(2)}) async-start(bf16[256,64,256]{2,1,0:T(8,128)(2,1)} %copy.1241), calls=%async_computation.1 | async-start | bytes 16777216 | tf_op jit(solution)/shard_map/all_to_all | solution.py:131
  1387.0 52.7 %all-to-all-start.3 = ((bf16[64,256,128]{2,0,1:T(8,128)(2,1)}), bf16[64,256,128]{2,0,1:T(8,128)(2,1)}, u32[]{:S(2)}, u32[]{:S(2)}) async-start(bf16[64,256,128]{2,0,1:T(8,128)(2,1)} %copy.1286), calls=%async_computation.3 | async-start | bytes 8388608 | tf_op jit(solution)/shard_map/all_to_all | solution.py:105
  1392.1 100.0 %copy-start.61 = (pred[64,256]{1,0:T(8,128)(4,1)}, pred[64,256]{1,0:T(8,128)(4,1)S(1)}, u32[]{:S(2)}) copy-start(pred[64,256]{1,0:T(8,128)(4,1)S(1)} %compare_bitcast_fusion) | copy-start | bytes 49156
  1565.7 52.7 %all-to-all-start.4 = ((bf16[256,64,128]{2,1,0:T(8,128)(2,1)}), bf16[256,64,128]{2,1,0:T(8,128)(2,1)}, u32[]{:S(2)}, u32[]{:S(2)}) async-start(bf16[256,64,128]{2,1,0:T(8,128)(2,1)} %copy.1295), calls=%async_computation.4 | async-start | bytes 8388608 | tf_op jit(solution)/shard_map/all_to_all | solution.py:108
  1570.5 183.7 %all-gather.17.cloned.1.call-start = ((), (), s32[]{:S(2)}) async-start(), calls=%async_computation.14 | async-start | bytes 1310720 | tf_op jit(solution)/shard_map/all_gather | solution.py:122
  1655.8 18.2 copy-start.82
  1678.0 708.3 %all-gather.19.cloned.1.call-start = ((), (), s32[]{:S(2)}) async-start(), calls=%async_computation.15 | async-start | bytes 5242880 | tf_op jit(solution)/shard_map/all_gather | solution.py:64
  2280.6 17.7 copy-start.70
  2354.4 244.5 %all-gather.21.cloned.1.call-start = ((), (), s32[]{:S(2)}) async-start(), calls=%async_computation.16 | async-start | bytes 20971520 | tf_op jit(solution)/shard_map/all_gather | solution.py:96
  2406.9 31.3 copy-start.54
  2452.9 18.3 copy-start.17
  2494.5 347.6 %all-gather.23.cloned.1.call-start = ((), (), s32[]{:S(2)}) async-start(), calls=%async_computation.17 | async-start | bytes 20971520 | tf_op jit(solution)/shard_map/all_gather | solution.py:101
  2651.1 18.4 copy-start.15
  2991.7 52.7 %all-to-all-start.8 = ((bf16[64,256,128]{2,0,1:T(8,128)(2,1)}), bf16[64,256,128]{2,0,1:T(8,128)(2,1)}, u32[]{:S(2)}, u32[]{:S(2)}) async-start(bf16[64,256,128]{2,0,1:T(8,128)(2,1)} %copy.1369), calls=%async_computation.8 | async-start | bytes 8388608 | tf_op jit(solution)/shard_map/all_to_all | solution.py:105
  3044.5 178.2 %all-to-all-start.6 = ((bf16[256,64,256]{2,1,0:T(8,128)(2,1)}), bf16[256,64,256]{2,1,0:T(8,128)(2,1)}, u32[]{:S(2)}, u32[]{:S(2)}) async-start(bf16[256,64,256]{2,1,0:T(8,128)(2,1)} %copy.1328), calls=%async_computation.6 | async-start | bytes 16777216 | tf_op jit(solution)/shard_map/all_to_all | solution.py:131
  3084.0 65.1 %copy-start.62 = (pred[64,256]{1,0:T(8,128)(4,1)S(1)}, pred[64,256]{1,0:T(8,128)(4,1)}, u32[]{:S(2)}) copy-start(pred[64,256]{1,0:T(8,128)(4,1)} %copy-done.61) | copy-start | bytes 49156
  3222.6 52.9 %all-to-all-start.9 = ((bf16[256,64,128]{2,1,0:T(8,128)(2,1)}), bf16[256,64,128]{2,1,0:T(8,128)(2,1)}, u32[]{:S(2)}, u32[]{:S(2)}) async-start(bf16[256,64,128]{2,1,0:T(8,128)(2,1)} %copy.1377), calls=%async_computation.9 | async-start | bytes 8388608 | tf_op jit(solution)/shard_map/all_to_all | solution.py:108
  (71 other events, 529.3 us)
Sparse Core Ops, SparseCore 0:
  22.7 16.5 all-gather.8
  710.3 32.6 all-gather.10
  851.1 104.1 all-gather.12
  1049.7 183.4 all-gather.14
  1678.1 13.9 all-gather.16
  2354.5 31.6 all-gather.18
  2494.7 104.1 all-gather.20
  2693.0 149.1 all-gather.22
where the time goes:
time: 3340 us; the launch traced here: 3320 us
  matrix products  1220 us (37%)
  local copies, waits for them, and re-layouts  759 us (23%)
  waiting for transfers between devices  568 us (17%)
  blocking collectives  389 us (12%)
  other arithmetic  334 us (10%)
  starting transfers between devices  42.6 us (1%)
    dot_general x32, matrix products, dense(): jnp.einsum('...c,cf->...f', x, weight, preferred_element_type=jnp.float32)  451 us
    sub x8, matrix products, attend(): attn_prob = jax.nn.softmax(logits, axis=-1).astype(jnp.bfloat16)  364 us
    dot_general x8, matrix products, attend(): jnp.einsum('bhqk,bkhd->bqhd', attn_prob, v_heads, preferred_element_type=...  304 us
    all_gather x4, waiting for transfers between devices, pair_stack(): right_full = lax.all_gather(right_act, GROUP_AXIS, axis=0, tiled=True)  301 us
    convert_element_type x18, local copies, waits for them, and re-layouts, residual(): return (x.astype(jnp.float32) + update).astype(jnp.bfloat16)  157 us
    slice x12, local copies, waits for them, and re-layouts, attend(): keyvals[..., :head_width].reshape(n_batch, k_len, num_heads, head_dim)  153 us
    all_to_all x1, blocking collectives, pair_stack(): left_cols = lax.all_to_all(left_act, GROUP_AXIS, 1, 0, tiled=True)  97.5 us
    all_to_all x1, blocking collectives, evoformer_block(): array_b7 = lax.all_to_all(value_a7, GROUP_AXIS, 1, 0, tiled=True)  97.2 us
  transfers between devices with their start and end apart: 16, of which 11 were waited for; matrix products, arithmetic and copies ran while one was open for 16% of the time, Pallas kernels for 0%

commit v1 on v0

v1 whole, which is shorter than its diff:
```python
import functools

import jax
import jax.numpy as jnp
from jax import lax
from jax.experimental import pallas as pl
from jax.experimental.pallas import tpu as pltpu
from jax.sharding import PartitionSpec as P

GROUP_AXIS = 'dap'
PARTS_AXIS = 'req'
MASKED_LOGIT = -1e9


def layer_norm(x):
    values = x.astype(jnp.float32)
    centered = values - jnp.mean(values, axis=-1, keepdims=True)
    variance = jnp.mean(centered * centered, axis=-1, keepdims=True)
    return (centered * lax.rsqrt(variance + 1e-5)).astype(jnp.bfloat16)


def residual(x, update):
    return (x.astype(jnp.float32) + update).astype(jnp.bfloat16)


def dense(x, weight):
    return jnp.einsum('...c,cf->...f', x, weight, preferred_element_type=jnp.float32)


LOG2E = 1.4426950408889634
HEAD_DIM = 32


def norm_rows(values):
    centered = values - jnp.mean(values, axis=-1, keepdims=True)
    variance = jnp.mean(centered * centered, axis=-1, keepdims=True)
    return (centered * lax.rsqrt(variance + 1e-5)).astype(jnp.bfloat16)


def mm(a, b):
    return jnp.dot(a, b, preferred_element_type=jnp.float32)


def attn_kernel(*refs, has_bias, has_transition):
    refs = list(refs)
    x_ref, mask_ref = refs[:2]
    refs = refs[2:]
    bias_ref = refs.pop(0) if has_bias else None
    w_ref, wo_ref = refs[:2]
    out_ref = refs[-1]
    width = wo_ref.shape[0]
    x = x_ref[0].astype(jnp.float32)
    proj = mm(norm_rows(x), w_ref[...]).astype(jnp.bfloat16)
    q, k, v = proj[:, :width], proj[:, width:2 * width], proj[:, 2 * width:3 * width]
    gate = jax.nn.sigmoid(proj[:, 3 * width:].astype(jnp.float32))
    kept = mask_ref[0] > 0
    lane_head = lax.broadcasted_iota(jnp.int32, (1, width), 1) // HEAD_DIM
    attended = None
    for h in range(width // HEAD_DIM):
        pick = jnp.where(lane_head == h, 1.0, 0.0).astype(jnp.bfloat16)
        logits = lax.dot_general(q * pick, k, (((1,), (1,)), ((), ())), preferred_element_type=jnp.float32)
        logits = logits * (HEAD_DIM ** -0.5 * LOG2E)
        if has_bias:
            logits = logits + bias_ref[h]
        logits = jnp.where(kept, logits, -1e9 * LOG2E)
        weight = jnp.exp2(logits - jnp.max(logits, axis=-1, keepdims=True))
        prob = (weight * (1.0 / jnp.sum(weight, axis=-1, keepdims=True))).astype(jnp.bfloat16)
        part = mm(prob, v * pick)
        attended = part if attended is None else attended + part
    gated = (attended * gate).astype(jnp.bfloat16)
    y = (x + mm(gated, wo_ref[...])).astype(jnp.bfloat16)
    if has_transition:
        y32 = y.astype(jnp.float32)
        hidden = jnp.maximum(mm(norm_rows(y32), refs[2][...]), 0.0).astype(jnp.bfloat16)
        y = (y32 + mm(hidden, refs[3][...])).astype(jnp.bfloat16)
    out_ref[0] = y


def attention(x, mask, w_qkvg, w_out, pair_bias=None, w_trans=None):
    n, length, width = x.shape
    args = [x, mask.astype(jnp.float32)[:, None, :]]
    specs = [pl.BlockSpec((1, length, width), lambda i: (i, 0, 0)), pl.BlockSpec((1, 1, length), lambda i: (i, 0, 0))]

    def whole(a):
        args.append(a)
        specs.append(pl.BlockSpec(a.shape, lambda i: (0,) * a.ndim))

    if pair_bias is not None:
        whole(pair_bias.astype(jnp.float32) * LOG2E)
    whole(w_qkvg)
    whole(w_out)
    for w in w_trans or ():
        whole(w)
    heads = w_out.shape[0] // HEAD_DIM
    flops = 2 * n * length * (width * w_qkvg.shape[1] + 2 * length * w_out.shape[0] + w_out.size)
    return pl.pallas_call(
        functools.partial(attn_kernel, has_bias=pair_bias is not None, has_transition=w_trans is not None),
        grid=(n,), in_specs=specs, out_specs=specs[0],
        out_shape=jax.ShapeDtypeStruct(x.shape, x.dtype),
        compiler_params=pltpu.CompilerParams(dimension_semantics=("arbitrary",), vmem_limit_bytes=48 << 20),
        cost_estimate=pl.CostEstimate(flops=flops, bytes_accessed=4 * x.size, transcendentals=n * heads * length * length),
    )(*args)


def pair_bias_full(pair_rows, w_bias):
    return lax.all_gather(head_bias(layer_norm(pair_rows), w_bias), GROUP_AXIS, axis=1, tiled=True)


def head_bias(pair_norm, w_bias):
    return jnp.einsum('ijc,ch->hij', pair_norm, w_bias, preferred_element_type=jnp.float32).astype(jnp.bfloat16)


def outer_update(array_b7, res_mask, full_mask, w_proj, w_out):
    opm_dim = w_proj.shape[1] // 2
    projected = dense(layer_norm(array_b7), w_proj).astype(jnp.bfloat16)
    mask_bf = res_mask.T.astype(jnp.bfloat16)[:, :, None]
    left_act = projected[..., :opm_dim] * mask_bf
    right_act = projected[..., opm_dim:] * mask_bf
    right_full = lax.all_gather(right_act, GROUP_AXIS, axis=0, tiled=True)
    outer_prod = jnp.einsum('isc,jse->ijce', left_act, right_full, preferred_element_type=jnp.float32).astype(jnp.bfloat16)
    n_rows, n_cols = outer_prod.shape[:2]
    update = dense(outer_prod.reshape(n_rows, n_cols, opm_dim * opm_dim), w_out)
    overlap = jnp.einsum('si,sj->ij', res_mask.astype(jnp.float32), full_mask.astype(jnp.float32))
    return update / (1e-3 + overlap)[:, :, None]


def tri_gates(pair_rows, mask_rows, w_proj):
    tri_dim = (w_proj.shape[1] - pair_rows.shape[-1]) // 4
    projected = dense(layer_norm(pair_rows), w_proj)
    mask_f = mask_rows.astype(jnp.float32)[:, :, None]
    left_act = (mask_f * jax.nn.sigmoid(projected[..., 2 * tri_dim:3 * tri_dim]) * projected[..., :tri_dim]).astype(jnp.bfloat16)
    right_act = (mask_f * jax.nn.sigmoid(projected[..., 3 * tri_dim:4 * tri_dim]) * projected[..., tri_dim:2 * tri_dim]).astype(jnp.bfloat16)
    gate_act = jax.nn.sigmoid(projected[..., 4 * tri_dim:])
    return left_act, right_act, gate_act


def tri_finish(product, gate_act, w_out):
    return gate_act * dense(layer_norm(product), w_out)


def pair_stack(pair_loc, pair_mask, pair_mask_t, pair_w):
    (tmo_proj, tmo_out, tmi_proj, tmi_out, tas_qkvg, tas_bias, tas_out,
     tae_qkvg, tae_bias, tae_out, ptr_in, ptr_out) = pair_w
    left_act, right_act, gate_act = tri_gates(pair_loc, pair_mask, tmo_proj)
    right_full = lax.all_gather(right_act, GROUP_AXIS, axis=0, tiled=True)
    product = jnp.einsum('ikc,jkc->ijc', left_act, right_full, preferred_element_type=jnp.float32)
    pair_loc = residual(pair_loc, tri_finish(product, gate_act, tmo_out))
    left_act, right_act, gate_act = tri_gates(pair_loc, pair_mask, tmi_proj)
    left_cols = lax.all_to_all(left_act, GROUP_AXIS, 1, 0, tiled=True)
    right_full = lax.all_gather(right_act, GROUP_AXIS, axis=0, tiled=True)
    product = jnp.einsum('kic,kjc->ijc', left_cols, right_full, preferred_element_type=jnp.float32)
    pair_loc = residual(pair_loc, tri_finish(product, gate_act, tmi_out))
    pair_loc = attention(pair_loc, pair_mask, tas_qkvg, tas_out, pair_bias_full(pair_loc, tas_bias))
    pair_cols = lax.all_to_all(pair_loc, GROUP_AXIS, 1, 0, tiled=True)
    pair_t = jnp.swapaxes(pair_cols, 0, 1)
    pair_t = attention(pair_t, pair_mask_t, tae_qkvg, tae_out, pair_bias_full(pair_t, tae_bias), (ptr_in, ptr_out))
    return jnp.swapaxes(lax.all_to_all(pair_t, GROUP_AXIS, 1, 0, tiled=True), 0, 1)


def evoformer_block(value_a7, pair_loc, full_mask, full_pair_mask, layer_w):
    (row_qkvg, row_bias, row_out, col_qkvg, col_out, mtr_in, mtr_out, opm_proj, opm_out) = layer_w[:9]
    shard_idx = lax.axis_index(GROUP_AXIS)
    seq_loc = value_a7.shape[0]
    res_loc = pair_loc.shape[0]
    seq_mask = lax.dynamic_slice_in_dim(full_mask, shard_idx * seq_loc, seq_loc, 0)
    res_mask = lax.dynamic_slice_in_dim(full_mask, shard_idx * res_loc, res_loc, 1)
    pair_mask = lax.dynamic_slice_in_dim(full_pair_mask, shard_idx * res_loc, res_loc, 0)
    pair_mask_t = lax.dynamic_slice_in_dim(full_pair_mask, shard_idx * res_loc, res_loc, 1).T
    value_a7 = attention(value_a7, seq_mask, row_qkvg, row_out, pair_bias_full(pair_loc, row_bias))
    array_b7 = jnp.swapaxes(lax.all_to_all(value_a7, GROUP_AXIS, 1, 0, tiled=True), 0, 1)
    array_b7 = attention(array_b7, res_mask.T, col_qkvg, col_out, None, (mtr_in, mtr_out))
    pair_loc = residual(pair_loc, outer_update(array_b7, res_mask, full_mask, opm_proj, opm_out))
    value_a7 = jnp.swapaxes(lax.all_to_all(array_b7, GROUP_AXIS, 1, 0, tiled=True), 0, 1)
    pair_loc = pair_stack(pair_loc, pair_mask, pair_mask_t, layer_w[9:])
    return value_a7, pair_loc


def solution(mesh):
    row_spec = P((PARTS_AXIS, GROUP_AXIS))

    def local_body(value_a7, pair_loc, value_a12, pair_mask_loc, *weights):
        full_mask = lax.all_gather(value_a12, GROUP_AXIS, axis=0, tiled=True)
        full_pair_mask = lax.all_gather(pair_mask_loc, GROUP_AXIS, axis=0, tiled=True)
        for layer_idx in range(weights[0].shape[0]):
            layer_w = tuple(weight[layer_idx] for weight in weights)
            value_a7, pair_loc = evoformer_block(value_a7, pair_loc, full_mask, full_pair_mask, layer_w)
        return value_a7, pair_loc

    def run_blocks(*arrays):
        n_weights = len(arrays) - 4
        return jax.shard_map(local_body, mesh=mesh, in_specs=(row_spec,) * 4 + (P(),) * n_weights, out_specs=(row_spec, row_spec), check_vma=False)(*arrays)

    return run_blocks
```

time: 3340 us -> 3010 us (0.901)
  Pallas kernels: 0 us -> 1100 us
  matrix products: 1220 us -> 268 us
  local copies, waits for them, and re-layouts: 759 us -> 329 us
  other arithmetic: 334 us -> 172 us
  waiting for transfers between devices: 568 us -> 660 us
    pallas_call x0 -> x8, Pallas kernels: none -> 1100 us  [attention(): pl.pallas_call(functools.partial(attn_kernel, has_bias=pair_bias is not N...]
    sub x8 -> x0, matrix products: 364 us -> none  [attend(): attn_prob = jax.nn.softmax(logits, axis=-1).astype(jnp.bfloat16)]
    dot_general x10 -> x2, matrix products: 345 us -> 38.5 us  [outer_update(): jnp.einsum('isc,jse->ijce', left_act, right_full, preferred_element_type=...]
    dot_general x32 -> x12, matrix products: 451 us -> 154 us  [dense(): jnp.einsum('...c,cf->...f', x, weight, preferred_element_type=jnp.float32)]
    slice x20 -> x0, local copies, waits for them, and re-layouts: 248 us -> none  [the longest x12 153 us: attend(): keyvals[..., :head_width].reshape(n_batch, k_len, num_heads, head_dim)]
    convert_element_type x33 -> x3, local copies, waits for them, and re-layouts: 264 us -> 65.9 us  [the longest x2 62.7 us: outer_update(): jnp.einsum('isc,jse->ijce', left_act, right_full, preferred_element_type=...]
    all_to_all x5, waiting for transfers between devices: 45.8 us -> 156 us  [the longest x2 79.9 us: evoformer_block(): lax.all_to_all(array_b7, GROUP_AXIS, 1, 0, tiled=True)]
    reshape x4 -> x0, local copies, waits for them, and re-layouts: 70 us -> none  [attend(): attended.reshape(n_batch, q_len, head_width)]
  transfers between devices with their start and end apart: 16 -> 16, of which waited for: 11 -> 13; matrix products, arithmetic and copies ran while one was open for 16% -> 5% of each run, Pallas kernels for 0% -> 4%
where the time goes in v1:
time: 3010 us; the launch traced here: 3000 us
  Pallas kernels  1100 us (37%)
  waiting for transfers between devices  660 us (22%)
  blocking collectives  414 us (14%)
  local copies, waits for them, and re-layouts  329 us (11%)
  matrix products  268 us (9%)
  other arithmetic  172 us (6%)
  starting transfers between devices  42.3 us (1%)
    pallas_call x8, Pallas kernels, attention(): pl.pallas_call(functools.partial(attn_kernel, has_bias=pair_bias is not N...  1100 us
    all_gather x4, waiting for transfers between devices, pair_stack(): right_full = lax.all_gather(right_act, GROUP_AXIS, axis=0, tiled=True)  260 us
    dot_general x12, matrix products, dense(): jnp.einsum('...c,cf->...f', x, weight, preferred_element_type=jnp.float32)  154 us
    all_gather x4, blocking collectives, pair_bias_full(): lax.all_gather(head_bias(layer_norm(pair_rows), w_bias), GROUP_AXIS, axis...  110 us
    all_to_all x1, blocking collectives, evoformer_block(): lax.all_to_all(value_a7, GROUP_AXIS, 1, 0, tiled=True)  101 us
    all_gather x1, blocking collectives, local_body(): lax.all_gather(pair_mask_loc, GROUP_AXIS, axis=0, tiled=True)  96.1 us
    all_to_all x1, blocking collectives, pair_stack(): left_cols = lax.all_to_all(left_act, GROUP_AXIS, 1, 0, tiled=True)  94.3 us
    all_to_all x1, waiting for transfers between devices, pair_stack(): left_cols = lax.all_to_all(left_act, GROUP_AXIS, 1, 0, tiled=True)  93.1 us
  transfers between devices with their start and end apart: 16, of which 13 were waited for; matrix products, arithmetic and copies ran while one was open for 5% of the time, Pallas kernels for 4%

profile of v1, /device:TPU:0, one launch (start us, length us, event | category | flops | bytes accessed | tf_op | source)
XLA Modules:
  0.0 2999.4 jit_solution(2475434111239135697)
XLA Ops:
  42.3 130.1 %shard_map.248 = bf16[64,256,256]{2,1,0:T(8,128)(2,1)} custom-call(bf16[64,256,256]{2,1,0:T(8,128)(2,1)} %refs_0_.1, f32[64,1,256]{2,1,0:T(1,128)S(1)} %broadcast_in_dim.8.refs_1_, f32[8,256,256]{2,1,0:T(8,128)S(1)} %convert_multiply_fusion.1.refs_2_, bf16[256,1024]{1,0:T(8,128)(2,1)S(1)} %get-tuple-element.21.refs_3_, ...), custom_call_target="tpu_custom_call" | custom-call | flops 15032385536 | bytes 16777216 | tf_op jit(solution)/shard_map/pallas_call | solution.py:96
  189.6 96.1 %all_gather.45 = s32[256,256]{1,0:T(8,128)S(1)} all-gather(s32[64,256]{1,0:T(8,128)S(1)} %copy-done.45), channel_id=1, replica_groups=mesh['req'=2,'dap'=4] {'dap'}, dimensions={0}, use_global_device_ids=true | all-gather | bytes 327680 | tf_op jit(solution)/shard_map/all_gather | solution.py:183
  299.2 191.3 %shard_map.249 = bf16[64,256,256]{2,1,0:T(8,128)(2,1)} custom-call(bf16[64,256,256]{2,1,0:T(8,128)(2,1)} %bitcast.298, f32[64,1,256]{2,1,0:T(1,128)S(1)} %copy-done.5, bf16[256,1024]{1,0:T(8,128)(2,1)S(1)} %copy-done, bf16[256,256]{1,0:T(8,128)(2,1)S(1)} %get-tuple-element.31.refs_3_, bf16[256,1024]{1,0:T(8,128)(2,1)S(1)} %get-tuple-element.17.refs_4_, ...), custom_call_target="tpu_custom_call" | custom-call | flops 15032385536 | bytes 16777216 | tf_op jit(solution)/shard_map/pallas_call | solution.py:96
  509.9 31.7 %all-gather.11.cloned.1.call-done = bf16[256,256,32]{1,2,0:T(8,128)(2,1)} async-done(((bf16[64,256,32]{1,2,0:T(8,128)(2,1)}), bf16[256,256,32]{1,2,0:T(8,128)(2,1)}) %all-gather.11.cloned.1.call-update) | async-done | bytes 4194320 | tf_op jit(solution)/shard_map/all_gather | solution.py:119
  560.0 31.3 %copy.197 = bf16[64,256,32,32]{1,3,2,0:T(8,128)(2,1)} copy(bf16[64,256,32,32]{1,0,2,3:T(8,128)(2,1)} %convert_bitcast_fusion.1) | data formatting | bytes 67108864 | tf_op jit(solution)/shard_map/convert_element_type | solution.py:120
  591.3 21.2 convert_reduce_fusion.5
  658.1 97.2 %all-gather.13.cloned.1.call-done = bf16[256,256,128]{2,1,0:T(8,128)(2,1)} async-done(((bf16[64,256,128]{2,1,0:T(8,128)(2,1)}), bf16[256,256,128]{2,1,0:T(8,128)(2,1)}) %all-gather.13.cloned.1.call-update) | async-done | bytes 16777232 | tf_op jit(solution)/shard_map/all_gather | solution.py:145
  755.3 21.9 copy.201
  854.1 93.1 %all-to-all-done.2 = bf16[64,256,128]{2,0,1:T(8,128)(2,1)} async-done(((bf16[64,256,128]{2,0,1:T(8,128)(2,1)}), bf16[64,256,128]{2,0,1:T(8,128)(2,1)}, u32[]{:S(2)}, u32[]{:S(2)}) %all-to-all-start.2) | async-done | bytes 4194336 | tf_op jit(solution)/shard_map/all_to_all | solution.py:149
  961.5 29.8 all-gather.15.cloned.1.call-done
  991.3 21.9 copy.209
  1056.2 100.1 %shard_map.250 = bf16[64,256,128]{2,1,0:T(8,128)(2,1)S(1)} custom-call(bf16[64,256,128]{2,1,0:T(8,128)(2,1)} %copy-done.23, f32[64,1,256]{2,1,0:T(1,128)S(1)} %broadcast_in_dim.10.refs_1_, f32[4,256,256]{2,1,0:T(8,128)S(1)} %convert_multiply_fusion.5.refs_2_, bf16[128,512]{1,0:T(8,128)(2,1)S(1)} %get-tuple-element.29.refs_3_, ...), custom_call_target="tpu_custom_call" | custom-call | flops 4831838208 | bytes 8388608 | tf_op jit(solution)/shard_map/pallas_call | solution.py:96
  1167.3 46.5 %all-to-all-done.3 = bf16[64,256,128]{2,0,1:T(8,128)(2,1)} async-done(((bf16[64,256,128]{2,0,1:T(8,128)(2,1)}), bf16[64,256,128]{2,0,1:T(8,128)(2,1)}, u32[]{:S(2)}, u32[]{:S(2)}) %all-to-all-start.3) | async-done | bytes 4194336 | tf_op jit(solution)/shard_map/all_to_all | solution.py:154
  1238.9 128.2 %shard_map.251 = bf16[64,256,128]{2,1,0:T(8,128)(2,1)S(1)} custom-call(bf16[64,256,128]{2,1,0:T(8,128)(2,1)} %bitcast.288, f32[64,1,256]{2,1,0:T(1,128)S(1)} %broadcast_in_dim.11.refs_1_, f32[4,256,256]{2,1,0:T(8,128)S(1)} %convert_multiply_fusion.4.refs_2_, bf16[128,512]{1,0:T(8,128)(2,1)S(1)} %get-tuple-element.64.refs_3_, ...), custom_call_target="tpu_custom_call" | custom-call | flops 4831838208 | bytes 8388608 | tf_op jit(solution)/shard_map/pallas_call | solution.py:96
  1388.2 36.3 %all-to-all-done.4 = bf16[64,256,128]{2,0,1:T(8,128)(2,1)} async-done(((bf16[64,256,128]{2,0,1:T(8,128)(2,1)}), bf16[64,256,128]{2,0,1:T(8,128)(2,1)}, u32[]{:S(2)}, u32[]{:S(2)}) %all-to-all-start.4) | async-done | bytes 4194336 | tf_op jit(solution)/shard_map/all_to_all | solution.py:157
  1448.8 79.9 %all-to-all-done.1 = bf16[64,256,256]{2,0,1:T(8,128)(2,1)} async-done(((bf16[64,256,256]{2,0,1:T(8,128)(2,1)}), bf16[64,256,256]{2,0,1:T(8,128)(2,1)}, u32[]{:S(2)}, u32[]{:S(2)}) %all-to-all-start.1) | async-done | bytes 8388640 | tf_op jit(solution)/shard_map/all_to_all | solution.py:173
  1538.6 130.1 %shard_map.252 = bf16[64,256,256]{2,1,0:T(8,128)(2,1)} custom-call(bf16[64,256,256]{2,1,0:T(8,128)(2,1)} %bitcast.296, f32[64,1,256]{2,1,0:T(1,128)S(1)} %copy-done.4, f32[8,256,256]{2,1,0:T(8,128)S(1)} %convert_multiply_fusion.refs_2_, bf16[256,1024]{1,0:T(8,128)(2,1)S(1)} %get-tuple-element.20.refs_3_, bf16[256,256]{1,0:T(8,128)(2,1)S(1)} %get-tuple-element.32.refs_4_), custom_call_target="tpu_custom_call" | custom-call | flops 15032385536 | bytes 16777216 | tf_op jit(solution)/shard_map/pallas_call | solution.py:96
  1680.3 100.7 %all_to_all.171 = bf16[64,256,256]{2,0,1:T(8,128)(2,1)} all-to-all(bf16[64,256,256]{2,0,1:T(8,128)(2,1)} %copy.222), channel_id=1, replica_groups=mesh['req'=2,'dap'=4] {'dap'}, dimensions={1} | all-to-all | bytes 16777216 | tf_op jit(solution)/shard_map/all_to_all | solution.py:170
  1789.4 190.7 %shard_map.253 = bf16[64,256,256]{2,1,0:T(8,128)(2,1)} custom-call(bf16[64,256,256]{2,1,0:T(8,128)(2,1)} %bitcast.297, f32[64,1,256]{2,1,0:T(1,128)S(1)} %copy-done.6, bf16[256,1024]{1,0:T(8,128)(2,1)S(1)} %get-tuple-element.63.refs_2_, bf16[256,256]{1,0:T(8,128)(2,1)S(1)} %get-tuple-element.30.refs_3_, bf16[256,1024]{1,0:T(8,128)(2,1)S(1)} %get-tuple-element.16.refs_4_, ...), custom_call_target="tpu_custom_call" | custom-call | flops 15032385536 | bytes 16777216 | tf_op jit(solution)/shard_map/pallas_call | solution.py:96
  1998.2 31.4 %all-gather.19.cloned.1.call-done = bf16[256,256,32]{1,2,0:T(8,128)(2,1)} async-done(((bf16[64,256,32]{1,2,0:T(8,128)(2,1)}), bf16[256,256,32]{1,2,0:T(8,128)(2,1)}) %all-gather.19.cloned.1.call-update) | async-done | bytes 4194320 | tf_op jit(solution)/shard_map/all_gather | solution.py:119
  2029.6 20.1 convert_bitcast_fusion
  2049.8 31.4 %copy.228 = bf16[64,256,32,32]{1,3,2,0:T(8,128)(2,1)} copy(bf16[64,256,32,32]{1,0,2,3:T(8,128)(2,1)} %convert_bitcast_fusion) | data formatting | bytes 67108864 | tf_op jit(solution)/shard_map/convert_element_type | solution.py:120
  2143.0 97.3 %all-gather.21.cloned.1.call-done = bf16[256,256,128]{2,1,0:T(8,128)(2,1)} async-done(((bf16[64,256,128]{2,1,0:T(8,128)(2,1)}), bf16[256,256,128]{2,1,0:T(8,128)(2,1)}) %all-gather.21.cloned.1.call-update) | async-done | bytes 16777232 | tf_op jit(solution)/shard_map/all_gather | solution.py:145
  2240.3 21.9 copy.232
  2332.4 94.3 %all_to_all.172 = bf16[64,256,128]{2,0,1:T(8,128)(2,1)S(1)} all-to-all(bf16[64,256,128]{2,0,1:T(8,128)(2,1)S(1)} %copy.237), channel_id=1, replica_groups=mesh['req'=2,'dap'=4] {'dap'}, dimensions={1} | all-to-all | bytes 8388608 | tf_op jit(solution)/shard_map/all_to_all | solution.py:149
  2438.8 36.2 %all-gather.23.cloned.1.call-done = bf16[256,256,128]{2,1,0:T(8,128)(2,1)} async-done(((bf16[64,256,128]{2,1,0:T(8,128)(2,1)}), bf16[256,256,128]{2,1,0:T(8,128)(2,1)}) %all-gather.23.cloned.1.call-update) | async-done | bytes 16777232 | tf_op jit(solution)/shard_map/all_gather | solution.py:150
  2475.0 21.9 copy.240
  2539.7 100.1 %shard_map.254 = bf16[64,256,128]{2,1,0:T(8,128)(2,1)S(1)} custom-call(bf16[64,256,128]{2,1,0:T(8,128)(2,1)} %copy-done.22, f32[64,1,256]{2,1,0:T(1,128)S(1)} %copy-done.2, f32[4,256,256]{2,1,0:T(8,128)S(1)} %convert_multiply_fusion.3.refs_2_, bf16[128,512]{1,0:T(8,128)(2,1)S(1)} %get-tuple-element.28.refs_3_, bf16[128,128]{1,0:T(8,128)(2,1)S(1)} %get-tuple-element.36.refs_4_), custom_call_target="tpu_custom_call" | custom-call | flops 4831838208 | bytes 8388608 | tf_op jit(solution)/shard_map/pallas_call | solution.py:96
  2661.0 36.3 %all-to-all-done.8 = bf16[64,256,128]{2,0,1:T(8,128)(2,1)} async-done(((bf16[64,256,128]{2,0,1:T(8,128)(2,1)}), bf16[64,256,128]{2,0,1:T(8,128)(2,1)}, u32[]{:S(2)}, u32[]{:S(2)}) %all-to-all-start.8) | async-done | bytes 4194336 | tf_op jit(solution)/shard_map/all_to_all | solution.py:154
  2719.0 82.4 %all_gather.55 = bf16[4,256,256]{2,1,0:T(8,128)(2,1)S(1)} all-gather(bf16[4,64,256]{2,1,0:T(8,128)(2,1)S(1)} %bitcast.307), channel_id=1, replica_groups=mesh['req'=2,'dap'=4] {'dap'}, dimensions={1}, use_global_device_ids=true | all-gather | bytes 655360 | tf_op jit(solution)/shard_map/all_gather | solution.py:106
  2801.5 127.8 %shard_map.255 = bf16[64,256,128]{2,1,0:T(8,128)(2,1)S(1)} custom-call(bf16[64,256,128]{2,1,0:T(8,128)(2,1)} %bitcast.286, f32[64,1,256]{2,1,0:T(1,128)S(1)} %broadcast_in_dim.11.refs_1_, f32[4,256,256]{2,1,0:T(8,128)S(1)} %convert_multiply_fusion.2.refs_2_, bf16[128,512]{1,0:T(8,128)(2,1)S(1)} %get-tuple-element.65.refs_3_, ...), custom_call_target="tpu_custom_call" | custom-call | flops 4831838208 | bytes 8388608 | tf_op jit(solution)/shard_map/pallas_call | solution.py:96
  2947.3 39.4 %all-to-all-done.9 = bf16[64,256,128]{2,0,1:T(8,128)(2,1)} async-done(((bf16[64,256,128]{2,0,1:T(8,128)(2,1)}), bf16[64,256,128]{2,0,1:T(8,128)(2,1)}, u32[]{:S(2)}, u32[]{:S(2)}) %all-to-all-start.9) | async-done | bytes 4194336 | tf_op jit(solution)/shard_map/all_to_all | solution.py:157
  (305 shorter events, 665.1 us)
Async XLA Ops:
  7.2 28.5 copy-start.40
  7.2 28.5 copy-start.28
  7.2 33.6 %all-gather.9.cloned.1.call-start = ((), (), s32[]{:S(2)}) async-start(), calls=%async_computation.10 | async-start | bytes 1310720 | tf_op jit(solution)/shard_map/all_gather | solution.py:106
  35.6 250.1 %copy-start.26 = (s32[256,256]{1,0:T(8,128)}, s32[256,256]{1,0:T(8,128)S(1)}, u32[]{:S(2)}) copy-start(s32[256,256]{1,0:T(8,128)S(1)} %all_gather.42) | copy-start | bytes 786436
  35.7 136.7 %copy-start.3 = (f32[64,1,256]{2,1,0:T(1,128)}, f32[64,1,256]{2,1,0:T(1,128)S(1)}, u32[]{:S(2)}) copy-start(f32[64,1,256]{2,1,0:T(1,128)S(1)} %broadcast_in_dim.8.refs_1_) | copy-start | bytes 196612
  183.8 104.1 %copy-start.41 = (bf16[2,256,256]{2,1,0:T(8,128)(2,1)S(1)}, bf16[2,256,256]{2,1,0:T(8,128)(2,1)}, u32[]{:S(2)}) copy-start(bf16[2,256,256]{2,1,0:T(8,128)(2,1)} %param.33) | copy-start | bytes 786436
  183.8 104.2 %copy-start.29 = (bf16[2,1024,256]{2,1,0:T(8,128)(2,1)S(1)}, bf16[2,1024,256]{2,1,0:T(8,128)(2,1)}, u32[]{:S(2)}) copy-start(bf16[2,1024,256]{2,1,0:T(8,128)(2,1)} %param.35) | copy-start | bytes 3145732
  183.8 106.8 %all-to-all-start = ((bf16[64,256,256]{2,0,1:T(8,128)(2,1)}), bf16[64,256,256]{2,0,1:T(8,128)(2,1)}, u32[]{:S(2)}, u32[]{:S(2)}) async-start(bf16[64,256,256]{2,0,1:T(8,128)(2,1)} %copy.190), calls=%async_computation | async-start | bytes 16777216 | tf_op jit(solution)/shard_map/all_to_all | solution.py:170
  189.6 352.0 %all-gather.11.cloned.1.call-start = ((), (), s32[]{:S(2)}) async-start(), calls=%async_computation.11 | async-start | bytes 5242880 | tf_op jit(solution)/shard_map/all_gather | solution.py:119
  508.9 246.4 %all-gather.13.cloned.1.call-start = ((), (), s32[]{:S(2)}) async-start(), calls=%async_computation.12 | async-start | bytes 20971520 | tf_op jit(solution)/shard_map/all_gather | solution.py:145
  509.8 344.2 %copy-start.24 = (f32[64,256]{1,0:T(8,128)}, f32[64,256]{1,0:T(8,128)S(1)}, u32[]{:S(2)}) copy-start(f32[64,256]{1,0:T(8,128)S(1)} %dynamic-slice_convert_fusion) | copy-start | bytes 196612
  509.9 81.3 %copy-start.48 = (f32[64,256]{1,0:T(8,128)}, f32[64,256]{1,0:T(8,128)S(1)}, u32[]{:S(2)}) copy-start(f32[64,256]{1,0:T(8,128)S(1)} %convolution_add_fusion) | copy-start | bytes 196612
  560.0 31.3 %copy-start.52 = (bf16[2,1024,128]{2,1,0:T(8,128)(2,1)S(1)}, bf16[2,1024,128]{2,1,0:T(8,128)(2,1)}, u32[]{:S(2)}) copy-start(bf16[2,1024,128]{2,1,0:T(8,128)(2,1)} %param.37) | copy-start | bytes 1572868
  591.3 27.3 copy-start.34
  650.8 340.5 %all-gather.15.cloned.1.call-start = ((), (), s32[]{:S(2)}) async-start(), calls=%async_computation.13 | async-start | bytes 20971520 | tf_op jit(solution)/shard_map/all_gather | solution.py:150
  849.0 98.2 %all-to-all-start.2 = ((bf16[64,256,128]{2,0,1:T(8,128)(2,1)}), bf16[64,256,128]{2,0,1:T(8,128)(2,1)}, u32[]{:S(2)}, u32[]{:S(2)}) async-start(bf16[64,256,128]{2,0,1:T(8,128)(2,1)} %copy.206), calls=%async_computation.2 | async-start | bytes 8388608 | tf_op jit(solution)/shard_map/all_to_all | solution.py:149
  854.1 202.1 %copy-start.1 = (f32[64,1,256]{2,1,0:T(1,128)}, f32[64,1,256]{2,1,0:T(1,128)S(1)}, u32[]{:S(2)}) copy-start(f32[64,1,256]{2,1,0:T(1,128)S(1)} %broadcast_in_dim.10.refs_1_) | copy-start | bytes 196612
  1161.1 52.7 %all-to-all-start.3 = ((bf16[64,256,128]{2,0,1:T(8,128)(2,1)}), bf16[64,256,128]{2,0,1:T(8,128)(2,1)}, u32[]{:S(2)}, u32[]{:S(2)}) async-start(bf16[64,256,128]{2,0,1:T(8,128)(2,1)} %copy.215), calls=%async_computation.3 | async-start | bytes 8388608 | tf_op jit(solution)/shard_map/all_to_all | solution.py:154
  1217.4 21.4 copy-start.13
  1371.8 52.8 %all-to-all-start.4 = ((bf16[64,256,128]{2,0,1:T(8,128)(2,1)}), bf16[64,256,128]{2,0,1:T(8,128)(2,1)}, u32[]{:S(2)}, u32[]{:S(2)}) async-start(bf16[64,256,128]{2,0,1:T(8,128)(2,1)} %copy.219), calls=%async_computation.4 | async-start | bytes 8388608 | tf_op jit(solution)/shard_map/all_to_all | solution.py:157
  1424.6 104.1 %all-to-all-start.1 = ((bf16[64,256,256]{2,0,1:T(8,128)(2,1)}), bf16[64,256,256]{2,0,1:T(8,128)(2,1)}, u32[]{:S(2)}, u32[]{:S(2)}) async-start(bf16[64,256,256]{2,0,1:T(8,128)(2,1)} %copy.193), calls=%async_computation.1 | async-start | bytes 16777216 | tf_op jit(solution)/shard_map/all_to_all | solution.py:173
  1430.2 106.9 %all-gather.17.cloned.1.call-start = ((), (), s32[]{:S(2)}) async-start(), calls=%async_computation.14 | async-start | bytes 1310720 | tf_op jit(solution)/shard_map/all_gather | solution.py:106
  1448.7 580.9 %all-gather.19.cloned.1.call-start = ((), (), s32[]{:S(2)}) async-start(), calls=%async_computation.15 | async-start | bytes 5242880 | tf_op jit(solution)/shard_map/all_gather | solution.py:119
  1998.2 242.1 %all-gather.21.cloned.1.call-start = ((), (), s32[]{:S(2)}) async-start(), calls=%async_computation.16 | async-start | bytes 20971520 | tf_op jit(solution)/shard_map/all_gather | solution.py:145
  2049.8 31.4 %copy-start.49 = (f32[64,256]{1,0:T(8,128)S(1)}, f32[64,256]{1,0:T(8,128)}, u32[]{:S(2)}) copy-start(f32[64,256]{1,0:T(8,128)} %copy-done.48) | copy-start | bytes 196612
  2049.8 31.4 %copy-start.53 = (bf16[2,1024,128]{2,1,0:T(8,128)(2,1)S(1)}, bf16[2,1024,128]{2,1,0:T(8,128)(2,1)}, u32[]{:S(2)}) copy-start(bf16[2,1024,128]{2,1,0:T(8,128)(2,1)} %param.37) | copy-start | bytes 1572868
  2081.2 23.9 copy-start.35
  2135.9 339.1 %all-gather.23.cloned.1.call-start = ((), (), s32[]{:S(2)}) async-start(), calls=%async_computation.17 | async-start | bytes 20971520 | tf_op jit(solution)/shard_map/all_gather | solution.py:150
  2644.6 52.8 %all-to-all-start.8 = ((bf16[64,256,128]{2,0,1:T(8,128)(2,1)}), bf16[64,256,128]{2,0,1:T(8,128)(2,1)}, u32[]{:S(2)}, u32[]{:S(2)}) async-start(bf16[64,256,128]{2,0,1:T(8,128)(2,1)} %copy.246), calls=%async_computation.8 | async-start | bytes 8388608 | tf_op jit(solution)/shard_map/all_to_all | solution.py:154
  2697.4 236.6 %all-to-all-start.6 = ((bf16[64,256,256]{2,0,1:T(8,128)(2,1)}), bf16[64,256,256]{2,0,1:T(8,128)(2,1)}, u32[]{:S(2)}, u32[]{:S(2)}) async-start(bf16[64,256,256]{2,0,1:T(8,128)(2,1)} %copy.224), calls=%async_computation.6 | async-start | bytes 16777216 | tf_op jit(solution)/shard_map/all_to_all | solution.py:173
  2706.8 94.5 %copy-start.12 = (bf16[64,4,64,128]{3,0,1,2:T(8,128)(2,1)}, bf16[64,4,64,128]{3,0,1,2:T(8,128)(2,1)S(1)}, u32[]{:S(2)}) copy-start(bf16[64,4,64,128]{3,0,1,2:T(8,128)(2,1)S(1)} %copy.247) | copy-start | bytes 12582916
  2934.0 52.8 %all-to-all-start.9 = ((bf16[64,256,128]{2,0,1:T(8,128)(2,1)}), bf16[64,256,128]{2,0,1:T(8,128)(2,1)}, u32[]{:S(2)}, u32[]{:S(2)}) async-start(bf16[64,256,128]{2,0,1:T(8,128)(2,1)} %copy.249), calls=%async_computation.9 | async-start | bytes 8388608 | tf_op jit(solution)/shard_map/all_to_all | solution.py:157
  (48 other events, 435.7 us)
Sparse Core Ops, SparseCore 0:
  23.6 17.2 all-gather.8
  509.0 32.5 all-gather.10
  650.9 104.3 all-gather.12
  842.2 149.1 all-gather.14
  1448.9 20.8 all-gather.16
  1998.3 31.2 all-gather.18
  2136.0 104.2 all-gather.20
  2327.6 147.3 all-gather.22
